TPU v7x, 32 devices: a whole 2x2x4 slice. The times are simulated.
32 devices in a mesh: ent: 16 (over z, y, x), grp: 2 (over core).
Axes of the slice: x: 2, y: 2, z: 4, core: 2. Of those that a mesh axis runs over, the one named last changes fastest.
Arguments:
- entity_table: bfloat16 [8192, 1024], P('ent'), may hold values from -2.5 to 2.5
- rel_phases: float32 [822, 512], replicated, may hold values from -3.1416 to 3.1416
- head_ids: int32 [8192], P(('ent', 'grp')), may hold values from 0 to 511
- rel_ids: int32 [8192], P(('ent', 'grp')), may hold values from 0 to 821
- target_pos: int32 [8192], P(('ent', 'grp')), may hold values from 0 to 511
- block_owner: int32 [4], replicated, may hold values from 0 to 15
- block_local: int32 [4], replicated, may hold values from 0 to 3
Outputs:
- losses: float32 [8192], P(('ent', 'grp'))
- head_grad: bfloat16 [8192, 1024], P(('ent', 'grp'))
- table_grad: bfloat16 [8192, 1024], P('ent')
- rel_grad: float32 [822, 512], replicated
Inputs may be any that keep to these rules, and one draw needn't show every extreme that they name: query q on device d (ent then grp) has head row (d // 2) * 512 + head_ids[q]. `target_pos`: position among the 512 candidates, block after block. Block b covers table rows from (block_owner[b] * 4 + block_local[b]) * 128 on; blocks may repeat.
All inputs are finite; a program needn't handle non-finite values.
Results may differ from a plain program's by a relative error of at most 0.0057.
Values may be sent and summed in bfloat16 or wider, within the bound.
A program may use at most 64 MiB of HBM per device.

v0:
```python
import jax
import jax.numpy as jnp
from jax import lax
from jax.sharding import PartitionSpec as P

BLK = 128
SOFTMAX_TEMPER = 2.0


def spread(block, axis, source):
    block = jnp.where(lax.axis_index(axis) == source, block, jnp.zeros_like(block))
    return lax.psum(block, axis)


def body(entity_table, rel_phases, head_ids, rel_ids, target_pos, block_owner, block_local):
    half_dim = rel_phases.shape[1]
    rel_count = rel_phases.shape[0]
    shard_rows = entity_table.shape[0]
    blocks_total = block_owner.shape[0]
    blank = jnp.zeros((blocks_total, BLK, 2 * half_dim), jnp.bfloat16)
    share = blocks_total // lax.axis_size("grp")
    offset = lax.axis_index("grp") * share

    def fetch_share(position, buffer):
        wanted = offset + position
        own_block = lax.dynamic_slice_in_dim(entity_table, block_local[wanted] * BLK, BLK, 0)
        arrived = spread(own_block, "ent", block_owner[wanted])
        return lax.dynamic_update_slice_in_dim(buffer, arrived[None], position, 0)

    halves = lax.fori_loop(0, share, fetch_share, blank[:share])
    fetched = lax.all_gather(halves, "grp", axis=0, tiled=True)
    candidate_block = fetched.reshape(blocks_total * BLK, 2 * half_dim)
    heads = jnp.take(entity_table, head_ids, axis=0).astype(jnp.float32)
    angles = jnp.take(rel_phases, rel_ids, axis=0)
    cosine = jnp.cos(angles)
    sine = jnp.sin(angles)
    real_head = heads[:, :half_dim]
    imag_head = heads[:, half_dim:]
    real_query = real_head * cosine - imag_head * sine
    imag_query = real_head * sine + imag_head * cosine
    query_reduced_precision = jnp.concatenate([real_query, imag_query], axis=1).astype(jnp.bfloat16)
    candidate_norm = jnp.sum(jnp.square(candidate_block.astype(jnp.float32)), axis=1)
    inner_products = lax.dot_general(
        query_reduced_precision,
        candidate_block,
        (((1,), (1,)), ((), ())),
        preferred_element_type=jnp.float32,
    )
    logit_scores = (2.0 * inner_products - candidate_norm[None, :]) / SOFTMAX_TEMPER
    top = jnp.max(logit_scores, axis=1, keepdims=True)
    log_total = top[:, 0] + jnp.log(jnp.sum(jnp.exp(logit_scores - top), axis=1))
    picked = jnp.take_along_axis(logit_scores, target_pos[:, None], axis=1)[:, 0]
    losses = log_total - picked
    columns = jnp.arange(logit_scores.shape[1], dtype=jnp.int32)
    onehot = (columns[None, :] == target_pos[:, None]).astype(jnp.float32)
    softmax_weights = jnp.exp(logit_scores - log_total[:, None]) - onehot
    weights_reduced_precision = softmax_weights.astype(jnp.bfloat16)
    query_gradient = (
        2.0
        / SOFTMAX_TEMPER
        * jnp.dot(weights_reduced_precision, candidate_block, preferred_element_type=jnp.float32)
    )
    back_products = lax.dot_general(
        weights_reduced_precision,
        query_reduced_precision,
        (((0,), (0,)), ((), ())),
        preferred_element_type=jnp.float32,
    )
    candidate_gradient = (
        2.0
        / SOFTMAX_TEMPER
        * (
            back_products
            - jnp.sum(softmax_weights, axis=0)[:, None] * candidate_block.astype(jnp.float32)
        )
    )
    real_grad = query_gradient[:, :half_dim]
    imag_grad = query_gradient[:, half_dim:]
    head_grad = jnp.concatenate(
        [real_grad * cosine + imag_grad * sine, imag_grad * cosine - real_grad * sine], axis=1
    ).astype(jnp.bfloat16)
    angle_grad = imag_grad * real_query - real_grad * imag_query
    rel_part = jax.ops.segment_sum(angle_grad, rel_ids, num_segments=rel_count)
    summed, rel_grad = lax.psum((candidate_gradient, rel_part), ("ent", "grp"))
    block_numbers = jnp.arange(shard_rows // BLK, dtype=jnp.int32)
    selector = (
        (block_owner == lax.axis_index("ent"))[:, None]
        & (block_local[:, None] == block_numbers[None, :])
    ).astype(jnp.float32)
    placed = jnp.einsum(
        "jb,jrk->brk",
        selector,
        summed.reshape(blocks_total, BLK, 2 * half_dim),
        precision=lax.Precision.HIGHEST,
    )
    table_grad = placed.reshape(shard_rows, 2 * half_dim).astype(jnp.bfloat16)
    return (losses, head_grad, table_grad, rel_grad)


def solution(mesh):
    return jax.shard_map(
        body,
        mesh=mesh,
        in_specs=(
            P("ent", None),
            P(),
            P(("ent", "grp")),
            P(("ent", "grp")),
            P(("ent", "grp")),
            P(),
            P(),
        ),
        out_specs=(P(("ent", "grp")), P(("ent", "grp"), None), P("ent", None), P()),
        check_vma=False,
    )
```

profile of v0, /device:TPU:0, one launch (start us, length us, event | category | flops | bytes accessed | tf_op | source)
XLA Modules:
  0.0 421.7 jit_solution(10624566232655944341)
XLA Ops:
  8.1 232.4 %while.13 = (s32[]{:T(128)}, bf16[2,128,1024]{2,1,0:T(8,128)(2,1)S(1)}, s32[]{:T(128)}, s32[4]{0:T(128)}, s32[4]{0:T(128)}, /*index=5*/bf16[512,1024]{1,0:T(8,12...) while((s32[]{:T(128)}, ...), condition=%wide.region_2.3_spmd, body=%wide.region_0.2_spmd.sunk | while | flops 262158 | bytes 2621779 | solution.py:30
  8.1 1.3 dynamic_slice.27
  9.5 1.2 dynamic_slice.26
  12.0 1.7 select_bitcast_fusion.2
  13.8 111.4 %all-reduce.6.cloned.1.call-done = bf16[1,128,1024]{2,1,0:T(8,128)(2,1)} async-done(((bf16[1,128,1024]{2,1,0:T(8,128)(2,1)}), bf16[1,128,1024]{2,1,0:T(8,128)(2,1)}) %all-reduce.6.cloned.1.call-update) | async-done | bytes 262160 | tf_op jit(solution)/shard_map/while/body/eval_jaxpr/psum | solution.py:12
  125.2 1.0 constant_dynamic-update-slice_fusion.2
  126.2 1.2 dynamic_slice.27
  127.4 1.2 dynamic_slice.26
  130.0 1.7 select_bitcast_fusion.2
  131.7 107.8 %all-reduce.6.cloned.1.call-done = bf16[1,128,1024]{2,1,0:T(8,128)(2,1)} async-done(((bf16[1,128,1024]{2,1,0:T(8,128)(2,1)}), bf16[1,128,1024]{2,1,0:T(8,128)(2,1)}) %all-reduce.6.cloned.1.call-update) | async-done | bytes 262160 | tf_op jit(solution)/shard_map/while/body/eval_jaxpr/psum | solution.py:12
  239.5 1.0 constant_dynamic-update-slice_fusion.2
  240.5 0.7 copy-done.8
  241.5 2.9 gather_fusion
  244.4 1.0 gather_fusion.1
  245.5 3.2 fusion.25
  248.7 2.3 all-gather.2.cloned.1.call-done
  251.0 1.5 multiply_reduce_fusion
  252.5 1.9 fusion.27
  254.5 2.3 gather_fusion.2
  257.1 0.6 fusion.14
  257.8 1.5 fusion.23
  259.4 0.6 multiply_subtract_fusion
  260.0 2.7 copy.14
  262.7 3.9 scatter_custom_fusion
  266.7 0.6 copy-done.13
  267.3 0.4 copy-done.4
  267.7 2.3 add_convert_fusion
  270.0 0.9 pad_maximum_fusion.1
  270.8 137.1 %all-reduce.4.cloned.1.call-done = (f32[4,128,1024]{2,0,1:T(4,128)}, f32[822,512]{1,0:T(8,128)}) async-done(((f32[4,128,1024]{2,0,1:T(4,128)}, f32[822,512]{1,0:T(8,128)}), (f32[4,128,1024]{2,0,1:T(4,128)}, f32[822,512]{1,0:T(8,128)})) %all-reduce.4.cloned.1.call-update) | async-done | bytes 3780624 | tf_op jit(solution)/shard_map/psum | solution.py:84
  407.9 3.8 convolution_convert_fusion
  411.8 1.3 copy.15
  413.1 1.2 copy.26
  (48 shorter events, 0.9 us)
Async XLA Ops:
  8.0 236.4 %copy-start = (f32[822,512]{1,0:T(8,128)S(1)}, f32[822,512]{1,0:T(8,128)}, u32[]{:S(2)}) copy-start(f32[822,512]{1,0:T(8,128)} %param.10) | copy-start | bytes 5050372
  8.0 233.3 %copy-start.11 = (s32[256]{0:T(256)S(1)}, s32[256]{0:T(256)}, u32[]{:S(2)}) copy-start(s32[256]{0:T(256)} %param.12) | copy-start | bytes 3076
  8.0 233.3 %copy-start.10 = (s32[256]{0:T(256)S(1)}, s32[256]{0:T(256)}, u32[]{:S(2)}) copy-start(s32[256]{0:T(256)} %param.11) | copy-start | bytes 3076
  8.1 233.3 %copy-start.9 = (s32[256]{0:T(256)S(1)}, s32[256]{0:T(256)}, u32[]{:S(2)}) copy-start(s32[256]{0:T(256)} %param.13) | copy-start | bytes 3076
  8.1 117.1 %all-reduce.6.cloned.1.call-start = ((), (), s32[]{:S(2)}) async-start(), calls=%async_computation.2 | async-start | bytes 524288 | tf_op jit(solution)/shard_map/while/body/eval_jaxpr/psum | solution.py:12
  126.1 113.3 %all-reduce.6.cloned.1.call-start = ((), (), s32[]{:S(2)}) async-start(), calls=%async_computation.2 | async-start | bytes 524288 | tf_op jit(solution)/shard_map/while/body/eval_jaxpr/psum | solution.py:12
  240.4 0.8 copy-start.8
  240.5 10.5 %all-gather.2.cloned.1.call-start = ((), (), s32[]{:S(2)}) async-start(), calls=%async_computation | async-start | bytes 1572864 | tf_op jit(solution)/shard_map/all_gather | solution.py:31
  241.3 166.7 %all-reduce.4.cloned.1.call-start = ((), (), s32[]{:S(2)}) async-start(), calls=%async_computation.1 | async-start | bytes 7569408 | tf_op jit(solution)/shard_map/psum | solution.py:84
  245.4 3.4 copy-start.3
  252.5 5.3 %copy-start.1 = (bf16[4,128,1024]{2,1,0:T(8,128)(2,1)S(1)}, bf16[4,128,1024]{2,1,0:T(8,128)(2,1)}, u32[]{:S(2)}) copy-start(bf16[4,128,1024]{2,1,0:T(8,128)(2,1)} %all-gather.2.cloned.1.call-done) | copy-start | bytes 3145732
  256.8 2.5 copy-start.7
  260.0 2.7 copy-start.2
  260.0 2.7 copy-start.5
  266.6 0.7 copy-start.13
  266.6 1.1 copy-start.4
  266.6 141.3 %copy-start.12 = (s32[4]{0:T(128)S(1)}, s32[4]{0:T(128)}, u32[]{:S(2)}) copy-start(s32[4]{0:T(128)} %get-tuple-element.239) | copy-start | bytes 52
  407.9 5.1 %copy-start.6 = (f32[822,512]{1,0:T(8,128)S(1)}, f32[822,512]{1,0:T(8,128)}, u32[]{:S(2)}) copy-start(f32[822,512]{1,0:T(8,128)} %get-tuple-element.219) | copy-start | bytes 5050372
Sparse Core Ops, SparseCore 0:
  14.7 110.4 all-reduce.5
  132.7 106.6 all-reduce.5
Sparse Core Ops, SparseCore 1:
  243.1 7.9 all-gather.1
  266.7 141.2 all-reduce.3
where the time goes:
time: 422 us
  waiting for transfers between devices  359 us (85%)
  local copies, waits for them, and re-layouts  20.2 us (5%)
  other arithmetic  16.4 us (4%)
  between operations  15.7 us (4%)
  matrix products  7.89 us (2%)
    psum x2, waiting for transfers between devices, spread(): return lax.psum(block, axis)  219 us
    psum x1, waiting for transfers between devices, body(): summed, rel_grad = lax.psum((candidate_gradient, rel_part), ('ent', 'grp'))  137 us
  transfers between devices with their start and end apart: 4, of which 4 were waited for; matrix products, arithmetic and copies ran while one was open for 2% of the time, Pallas kernels for 0%

commit v1 on v0

--- a/solution.py
+++ b/solution.py
@@ -9,7 +9,7 @@
 
 def spread(block, axis, source):
     block = jnp.where(lax.axis_index(axis) == source, block, jnp.zeros_like(block))
-    return lax.psum(block, axis)
+    return jnp.sum(lax.all_gather(block, axis), axis=0)
 
 
 def body(entity_table, rel_phases, head_ids, rel_ids, target_pos, block_owner, block_local):

time: 422 us -> 360 us (0.85)
  waiting for transfers between devices: 359 us -> 292 us
  other arithmetic: 16.4 us -> 22.6 us
    psum x2 -> x0, waiting for transfers between devices: 219 us -> none  [spread(): return lax.psum(block, axis)]
    all_gather x0 -> x2, waiting for transfers between devices: none -> 153 us  [spread(): return jnp.sum(lax.all_gather(block, axis), axis=0)]
    reduce_sum x0 -> x2, other arithmetic: none -> 6.25 us  [spread(): return jnp.sum(lax.all_gather(block, axis), axis=0)]
  transfers between devices with their start and end apart: 4 -> 4, of which waited for: 4 -> 4; matrix products, arithmetic and copies ran while one was open for 2% -> 3% of each run, Pallas kernels for 0% -> 0%
where the time goes in v1:
time: 360 us; the launch traced here: 359 us
  waiting for transfers between devices  292 us (81%)
  other arithmetic  22.6 us (6%)
  local copies, waits for them, and re-layouts  18.3 us (5%)
  between operations  15.7 us (4%)
  matrix products  7.9 us (2%)
    all_gather x2, waiting for transfers between devices, spread(): return jnp.sum(lax.all_gather(block, axis), axis=0)  153 us
    psum x1, waiting for transfers between devices, body(): summed, rel_grad = lax.psum((candidate_gradient, rel_part), ('ent', 'grp'))  137 us
  transfers between devices with their start and end apart: 4, of which 4 were waited for; matrix products, arithmetic and copies ran while one was open for 3% of the time, Pallas kernels for 0%

profile of v1, /device:TPU:0, one launch (start us, length us, event | category | flops | bytes accessed | tf_op | source)
XLA Modules:
  0.0 359.4 jit_solution(2186541311743715462)
XLA Ops:
  8.1 170.4 %while.15 = (s32[]{:T(128)}, bf16[2,128,1024]{2,1,0:T(8,128)(2,1)S(1)}, s32[]{:T(128)}, s32[4]{0:T(128)}, s32[4]{0:T(128)}, /*index=5*/bf16[512,1024]{1,0:T(8,12...) while((s32[]{:T(128)}, ...), condition=%wide.region_2.3_spmd, body=%wide.region_0.2_spmd.sunk | while | flops 2097166 | bytes 18874716 | solution.py:30
  8.1 1.3 dynamic_slice.36
  9.5 1.2 dynamic_slice.35
  12.0 1.7 dynamic-slice_select_fusion.2
  13.8 78.5 %all-gather.8.cloned.1.call-done = bf16[2048,1024]{1,0:T(8,128)(2,1)} async-done(((bf16[128,1024]{1,0:T(8,128)(2,1)}), bf16[2048,1024]{1,0:T(8,128)(2,1)}) %all-gather.8.cloned.1.call-update) | async-done | bytes 4194320 | tf_op jit(solution)/shard_map/while/body/eval_jaxpr/all_gather | solution.py:12
  92.2 3.1 reduce_sum.48
  95.5 1.2 dynamic_slice.36
  96.7 1.2 dynamic_slice.35
  99.2 1.7 dynamic-slice_select_fusion.2
  101.0 74.3 %all-gather.8.cloned.1.call-done = bf16[2048,1024]{1,0:T(8,128)(2,1)} async-done(((bf16[128,1024]{1,0:T(8,128)(2,1)}), bf16[2048,1024]{1,0:T(8,128)(2,1)}) %all-gather.8.cloned.1.call-update) | async-done | bytes 4194320 | tf_op jit(solution)/shard_map/while/body/eval_jaxpr/all_gather | solution.py:12
  175.3 3.1 reduce_sum.48
  178.6 0.7 copy-done.8
  179.5 2.9 gather_fusion
  182.4 1.0 gather_fusion.1
  183.6 3.2 fusion.25
  186.8 1.9 all-gather.6.cloned.1.call-done
  188.7 1.5 multiply_reduce_fusion
  190.2 2.0 fusion.27
  192.1 2.3 gather_fusion.2
  194.7 0.6 fusion.14
  195.5 1.5 fusion.23
  197.0 0.6 multiply_subtract_fusion
  197.6 2.7 copy.14
  200.3 3.9 %scatter_custom_fusion = f32[822,512]{1,0:T(8,128)} fusion(s32[256]{0:T(256)S(1)} %copy-done.11, f32[]{:T(128)} %constant.158.clone.1, f32[256,512]{1,0:T(8,128)} %get-tuple-element.182, f32[256,512]{1,0:T(8,128)S(1)} %copy-done.5, f32[256,1024]{1,0:T(8,128)S(1)} %copy-done.2), kind=kCustom, calls=%fused_computation.12 | custom fusion | flops 524288 | bytes 3780612 | tf_op jit(solution)/shard_map/scatter-add | solution.py:83
  204.3 0.6 copy-done.13
  204.9 0.4 copy-done.4
  205.3 2.3 add_convert_fusion
  207.6 0.9 pad_maximum_fusion.1
  208.5 137.1 %all-reduce.3.cloned.1.call-done = (f32[4,128,1024]{2,0,1:T(4,128)}, f32[822,512]{1,0:T(8,128)}) async-done(((f32[4,128,1024]{2,0,1:T(4,128)}, f32[822,512]{1,0:T(8,128)}), (f32[4,128,1024]{2,0,1:T(4,128)}, f32[822,512]{1,0:T(8,128)})) %all-reduce.3.cloned.1.call-update) | async-done | bytes 3780624 | tf_op jit(solution)/shard_map/psum | solution.py:84
  345.6 3.8 %convolution_convert_fusion = bf16[4,128,1024]{2,0,1:T(4,128)(2,1)S(1)} fusion(f32[4,128,1024]{2,0,1:T(4,128)} %get-tuple-element.171, s32[4]{0:T(128)S(1)} %copy-done.12, pred[4]{0:T(512)(128)(4,1)S(1)} %broadcast_compare_fusion), kind=kOutput, calls=%fused_computation.8 | convolution fusion | flops 25690144 | bytes 3145748 | tf_op jit(solution)/shard_map/jb,jrk->brk/dot_general | solution.py:90
  349.5 1.3 copy.15
  350.8 1.2 copy.25
  (50 shorter events, 1.0 us)
Async XLA Ops:
  8.0 174.4 %copy-start = (f32[822,512]{1,0:T(8,128)S(1)}, f32[822,512]{1,0:T(8,128)}, u32[]{:S(2)}) copy-start(f32[822,512]{1,0:T(8,128)} %param.10) | copy-start | bytes 5050372
  8.0 171.3 %copy-start.11 = (s32[256]{0:T(256)S(1)}, s32[256]{0:T(256)}, u32[]{:S(2)}) copy-start(s32[256]{0:T(256)} %param.12) | copy-start | bytes 3076
  8.0 171.4 %copy-start.10 = (s32[256]{0:T(256)S(1)}, s32[256]{0:T(256)}, u32[]{:S(2)}) copy-start(s32[256]{0:T(256)} %param.11) | copy-start | bytes 3076
  8.1 171.4 %copy-start.9 = (s32[256]{0:T(256)S(1)}, s32[256]{0:T(256)}, u32[]{:S(2)}) copy-start(s32[256]{0:T(256)} %param.13) | copy-start | bytes 3076
  8.1 84.1 %all-gather.8.cloned.1.call-start = ((), (), s32[]{:S(2)}) async-start(), calls=%async_computation.2 | async-start | bytes 4456448 | tf_op jit(solution)/shard_map/while/body/eval_jaxpr/all_gather | solution.py:12
  95.4 79.9 %all-gather.8.cloned.1.call-start = ((), (), s32[]{:S(2)}) async-start(), calls=%async_computation.2 | async-start | bytes 4456448 | tf_op jit(solution)/shard_map/while/body/eval_jaxpr/all_gather | solution.py:12
  178.5 0.8 copy-start.8
  178.5 10.1 %all-gather.6.cloned.1.call-start = ((), (), s32[]{:S(2)}) async-start(), calls=%async_computation | async-start | bytes 1572864 | tf_op jit(solution)/shard_map/all_gather | solution.py:31
  179.3 166.3 %all-reduce.3.cloned.1.call-start = ((), (), s32[]{:S(2)}) async-start(), calls=%async_computation.1 | async-start | bytes 7569408 | tf_op jit(solution)/shard_map/psum | solution.py:84
  183.4 3.4 copy-start.3
  190.2 5.3 %copy-start.1 = (bf16[4,128,1024]{2,1,0:T(8,128)(2,1)S(1)}, bf16[4,128,1024]{2,1,0:T(8,128)(2,1)}, u32[]{:S(2)}) copy-start(bf16[4,128,1024]{2,1,0:T(8,128)(2,1)} %all-gather.6.cloned.1.call-done) | copy-start | bytes 3145732
  194.5 2.5 copy-start.7
  197.6 2.7 copy-start.2
  197.6 2.7 copy-start.5
  204.3 0.7 copy-start.13
  204.3 1.1 copy-start.4
  204.3 141.3 %copy-start.12 = (s32[4]{0:T(128)S(1)}, s32[4]{0:T(128)}, u32[]{:S(2)}) copy-start(s32[4]{0:T(128)} %get-tuple-element.287) | copy-start | bytes 52
  345.6 5.1 %copy-start.6 = (f32[822,512]{1,0:T(8,128)S(1)}, f32[822,512]{1,0:T(8,128)}, u32[]{:S(2)}) copy-start(f32[822,512]{1,0:T(8,128)} %get-tuple-element.267) | copy-start | bytes 5050372
Sparse Core Ops, SparseCore 0:
  13.9 78.3 all-gather.7
  101.1 74.1 all-gather.7
Sparse Core Ops, SparseCore 1:
  181.1 7.5 all-gather.5
  204.4 141.2 all-reduce.2
